TPU v7x, 32 devices: a whole 2x2x4 slice. The times are simulated.
32 devices in a mesh: tensor: 4 (over x, core), dp: 4 (over z), ctx: 2 (over y).
Axes of the slice: x: 2, y: 2, z: 4, core: 2. Of those that a mesh axis runs over, the one named last changes fastest.
Arguments:
- inputs: bfloat16 [4, 1024, 2048], P('dp', 'ctx'), may hold values from -8 to 8
- cotangent: bfloat16 [4, 1024, 2048], P('dp', 'ctx'), may hold values from -6 to 6
- qkv_state: float32 [3, 2, 2048, 3, 2048], P(None, None, ('dp', 'ctx'), None, 'tensor'), may hold values from -1024 to 1024, as said below
- out_state: float32 [3, 2, 2048, 2048], P(None, None, 'tensor', ('dp', 'ctx')), may hold values from -1024 to 1024, as said below
- up_state: float32 [3, 2, 2048, 8192], P(None, None, ('dp', 'ctx'), 'tensor'), may hold values from -1024 to 1024, as said below
- down_state: float32 [3, 2, 8192, 2048], P(None, None, 'tensor', ('dp', 'ctx')), may hold values from -1024 to 1024, as said below
- qkv_bias_state: float32 [3, 2, 3, 2048], P(None, None, None, ('tensor', 'dp', 'ctx')), may hold values from -1024 to 1024, as said below
- up_bias_state: float32 [3, 2, 8192], P(None, None, ('tensor', 'dp', 'ctx')), may hold values from -1024 to 1024, as said below
- norm_state: float32 [3, 2, 5, 2048], P(None, None, None, ('dp', 'ctx')), may hold values from -1024 to 1024, as said below
Outputs:
- outputs: bfloat16 [4, 1024, 2048], P('dp', 'ctx')
- input_grad: float32 [4, 1024, 2048], P('dp', 'ctx')
- qkv_grad: float32 [3, 2, 2048, 3, 2048], P(None, None, ('dp', 'ctx'), None, 'tensor')
- qkv_new: float32 [2, 2048, 3, 2048], P(None, ('dp', 'ctx'), None, 'tensor')
- out_grad: float32 [3, 2, 2048, 2048], P(None, None, 'tensor', ('dp', 'ctx'))
- out_new: float32 [2, 2048, 2048], P(None, 'tensor', ('dp', 'ctx'))
- up_grad: float32 [3, 2, 2048, 8192], P(None, None, ('dp', 'ctx'), 'tensor')
- up_new: float32 [2, 2048, 8192], P(None, ('dp', 'ctx'), 'tensor')
- down_grad: float32 [3, 2, 8192, 2048], P(None, None, 'tensor', ('dp', 'ctx'))
- down_new: float32 [2, 8192, 2048], P(None, 'tensor', ('dp', 'ctx'))
- qkv_bias_grad: float32 [3, 2, 3, 2048], P(None, None, None, ('tensor', 'dp', 'ctx'))
- qkv_bias_new: float32 [2, 3, 2048], P(None, None, ('tensor', 'dp', 'ctx'))
- up_bias_grad: float32 [3, 2, 8192], P(None, None, ('tensor', 'dp', 'ctx'))
- up_bias_new: float32 [2, 8192], P(None, ('tensor', 'dp', 'ctx'))
- norm_grad: float32 [3, 2, 5, 2048], P(None, None, None, ('dp', 'ctx'))
- norm_new: float32 [2, 5, 2048], P(None, None, ('dp', 'ctx'))
Inputs may be any that keep to these rules, and one draw needn't show every extreme that they name: `qkv_state`: index 0 of the first dimension holds the weights, 1 the first moments, 2 the roots of the second moments, which are positive. `out_state`: index 0 of the first dimension holds the weights, 1 the first moments, 2 the roots of the second moments, which are positive. `up_state`: index 0 of the first dimension holds the weights, 1 the first moments, 2 the roots of the second moments, which are positive. `down_state`: index 0 of the first dimension holds the weights, 1 the first moments, 2 the roots of the second moments, which are positive. `qkv_bias_state`: index 0 of the first dimension holds the biases, 1 the first moments, 2 the roots of the second moments, which are positive. `up_bias_state`: index 0 of the first dimension holds the biases, 1 the first moments, 2 the roots of the second moments, which are positive. `norm_state`: index 0 of the first dimension holds the gains, shifts and output bias, 1 the first moments, 2 the roots of the second moments, which are positive.
All inputs are finite; a program needn't handle non-finite values.
Results may differ from a plain program's by a relative error of at most 0.015.
Values may be sent and summed in bfloat16 or wider, within the bound.
A program may use at most 384 MiB of HBM per device.

v0:
```python
import jax
import jax.numpy as jnp
from jax import lax
from jax.sharding import PartitionSpec as P

HEAD_DIM = 256
ROT = 64
STEP = 4
beta_one = 0.9
beta_two = 0.95
adam_eps = 1e-08
norm_eps = 1e-05
rate_matrix = 0.008
rate_vector = 0.2
weight_decay = 0.01


def layer_norm(values, norm_gain, norm_shift):
    centered = values - jnp.mean(values, axis=-1, keepdims=True)
    spread = jnp.mean(centered * centered, axis=-1, keepdims=True)
    return centered * lax.rsqrt(spread + norm_eps) * norm_gain + norm_shift


def angle_tables(positions, rotated):
    halfway = rotated // 2
    frequency = 10000.0 ** (-2.0 * jnp.arange(halfway, dtype=jnp.float32) / rotated)
    angles = positions[:, None] * frequency[None, :]
    return (jnp.cos(angles)[:, None, :], jnp.sin(angles)[:, None, :])


def rotate(features_in, cosine_table, sine_table):
    halfway = cosine_table.shape[-1]
    lower_half = features_in[..., :halfway]
    upper_half = features_in[..., halfway : 2 * halfway]
    return jnp.concatenate(
        [
            lower_half * cosine_table - upper_half * sine_table,
            upper_half * cosine_table + lower_half * sine_table,
            features_in[..., 2 * halfway :],
        ],
        axis=-1,
    )


def rotate_back(features_in, cosine_table, sine_table):
    halfway = cosine_table.shape[-1]
    lower_half = features_in[..., :halfway]
    upper_half = features_in[..., halfway : 2 * halfway]
    return jnp.concatenate(
        [
            lower_half * cosine_table + upper_half * sine_table,
            upper_half * cosine_table - lower_half * sine_table,
            features_in[..., 2 * halfway :],
        ],
        axis=-1,
    )


def adam_step(packed, gradient, learn_rate, decay_rate):
    moment = beta_one * packed[1] + (1.0 - beta_one) * gradient
    root_second = jnp.sqrt(
        beta_two * packed[2] * packed[2] + (1.0 - beta_two) * gradient * gradient
    )
    update = (
        learn_rate
        * (moment / (1.0 - beta_one**STEP))
        / (root_second / (1.0 - beta_two**STEP) ** 0.5 + adam_eps)
    )
    weight = packed[0] - update - learn_rate * decay_rate * packed[0]
    return (jnp.stack([gradient, moment, root_second]), weight)


def lowered(packed, layer_index):
    return packed[0, layer_index].astype(jnp.bfloat16)


def causal_scores(queries, key_block, ctx_place):
    row_span = queries.shape[1]
    length = key_block.shape[1]
    scores = jnp.einsum(
        "sqhd,skhd->shqk", queries, key_block, preferred_element_type=jnp.float32
    ) * HEAD_DIM ** (-0.5)
    query_pos = ctx_place * row_span + jnp.arange(row_span, dtype=jnp.int32)
    causal = jnp.arange(length, dtype=jnp.int32)[None, :] <= query_pos[:, None]
    return jnp.where(causal[None, None], scores, -1e30)


def forward_layer(hidden, weights, cosine_table, sine_table, ctx_place):
    qkv_weight, out_weight, up_weight, down_weight, bias_triple, up_bias, norm_rows = weights
    bias_full = bias_triple.astype(jnp.float32)
    norm_rows = norm_rows.astype(jnp.float32)
    sequences, row_span, features = hidden.shape
    local_width = qkv_weight.shape[2]
    head_count = local_width // HEAD_DIM
    normed_one = layer_norm(hidden, norm_rows[0], norm_rows[1]).astype(jnp.bfloat16)
    normed_two = layer_norm(hidden, norm_rows[2], norm_rows[3]).astype(jnp.bfloat16)
    projected = (
        jnp.einsum("scd,dkj->sckj", normed_one, qkv_weight, preferred_element_type=jnp.float32)
        + bias_full
    )
    projected = projected.reshape(sequences, row_span, 3, head_count, HEAD_DIM)
    queries = rotate(projected[:, :, 0], cosine_table, sine_table).astype(jnp.bfloat16)
    keys_here = rotate(projected[:, :, 1], cosine_table, sine_table).astype(jnp.bfloat16)
    values_here = projected[:, :, 2].astype(jnp.bfloat16)
    key_block, value_block = (
        lax.all_gather(keys_here, "ctx", axis=1, tiled=True),
        lax.all_gather(values_here, "ctx", axis=1, tiled=True),
    )
    scores = causal_scores(queries, key_block, ctx_place)
    row_peak = jnp.max(scores, axis=-1, keepdims=True)
    exponent = jnp.exp(scores - row_peak)
    row_total = jnp.sum(exponent, axis=-1, keepdims=True)
    attention = exponent / row_total
    log_total = row_peak + jnp.log(row_total)
    mixture = jnp.einsum(
        "shqk,skhd->sqhd",
        attention.astype(jnp.bfloat16),
        value_block,
        preferred_element_type=jnp.float32,
    )
    mixture = mixture.reshape(sequences, row_span, local_width).astype(jnp.bfloat16)
    pre_act = jnp.einsum(
        "scd,df->scf", normed_two, up_weight, preferred_element_type=jnp.float32
    ) + up_bias.astype(jnp.float32)
    activation = jax.nn.gelu(pre_act, approximate=False).astype(jnp.bfloat16)
    summand = jnp.einsum("scj,jd->scd", mixture, out_weight, preferred_element_type=jnp.float32)
    summand = summand + jnp.einsum(
        "scf,fd->scd", activation, down_weight, preferred_element_type=jnp.float32
    )
    branch = lax.psum(summand, "tensor")
    saved = (
        hidden,
        normed_one,
        normed_two,
        queries,
        key_block,
        value_block,
        log_total,
        mixture,
        pre_act,
        activation,
    )
    return (hidden + branch + norm_rows[4], saved)


def backward_layer(gradient, weights, stored, cosine_table, sine_table, ctx_place):
    qkv_weight, out_weight, up_weight, down_weight, bias_triple, up_bias, norm_rows = weights
    norm_rows = norm_rows.astype(jnp.float32)
    (
        hidden,
        normed_one,
        normed_two,
        queries,
        key_block,
        value_block,
        log_total,
        mixture,
        pre_act,
        activation,
    ) = stored
    sequences, row_span, features = gradient.shape
    local_width = qkv_weight.shape[2]
    head_count = local_width // HEAD_DIM
    grad_low = gradient.astype(jnp.bfloat16)
    grad_bias_sum = jnp.sum(gradient, axis=(0, 1))
    grad_out_w = jnp.einsum("scj,scd->jd", mixture, grad_low, preferred_element_type=jnp.float32)
    grad_down_w = jnp.einsum(
        "scf,scd->fd", activation, grad_low, preferred_element_type=jnp.float32
    )
    grad_mixture = jnp.einsum(
        "scd,jd->scj", grad_low, out_weight, preferred_element_type=jnp.float32
    ).astype(jnp.bfloat16)
    grad_activation = jnp.einsum(
        "scd,fd->scf", grad_low, down_weight, preferred_element_type=jnp.float32
    )
    unused_value, gelu_back = jax.vjp(
        lambda argument: jax.nn.gelu(argument, approximate=False), pre_act
    )
    grad_pre = gelu_back(grad_activation)[0].astype(jnp.bfloat16)
    grad_up_bias = jnp.sum(grad_pre.astype(jnp.float32), axis=(0, 1))
    grad_up_w = jnp.einsum("scd,scf->df", normed_two, grad_pre, preferred_element_type=jnp.float32)
    grad_normed_two = jnp.einsum(
        "scf,df->scd", grad_pre, up_weight, preferred_element_type=jnp.float32
    )
    grad_heads = grad_mixture.reshape(sequences, row_span, head_count, HEAD_DIM)
    scores = causal_scores(queries, key_block, ctx_place)
    attention = jnp.exp(scores - log_total)
    grad_attention = jnp.einsum(
        "sqhd,skhd->shqk", grad_heads, value_block, preferred_element_type=jnp.float32
    )
    row_delta = jnp.sum(attention * grad_attention, axis=-1, keepdims=True)
    grad_scores = (attention * (grad_attention - row_delta)).astype(jnp.bfloat16)
    score_scale = HEAD_DIM ** (-0.5)
    grad_queries = (
        jnp.einsum("shqk,skhd->sqhd", grad_scores, key_block, preferred_element_type=jnp.float32)
        * score_scale
    )
    key_terms = (
        jnp.einsum("shqk,sqhd->skhd", grad_scores, queries, preferred_element_type=jnp.float32)
        * score_scale
    )
    value_terms = jnp.einsum(
        "shqk,sqhd->skhd",
        attention.astype(jnp.bfloat16),
        grad_heads,
        preferred_element_type=jnp.float32,
    )
    grad_keys, grad_values = (
        lax.psum_scatter(
            key_terms.astype(jnp.bfloat16), "ctx", scatter_dimension=1, tiled=True
        ).astype(jnp.float32),
        lax.psum_scatter(
            value_terms.astype(jnp.bfloat16), "ctx", scatter_dimension=1, tiled=True
        ).astype(jnp.float32),
    )
    grad_projected = jnp.stack(
        [
            rotate_back(grad_queries, cosine_table, sine_table),
            rotate_back(grad_keys, cosine_table, sine_table),
            grad_values,
        ],
        axis=2,
    )
    grad_projected = grad_projected.reshape(sequences, row_span, 3, local_width).astype(
        jnp.bfloat16
    )
    grad_qkv_bias = jnp.sum(grad_projected.astype(jnp.float32), axis=(0, 1))
    grad_qkv_w = jnp.einsum(
        "scd,sckj->dkj", normed_one, grad_projected, preferred_element_type=jnp.float32
    )
    grad_normed_one = jnp.einsum(
        "sckj,dkj->scd", grad_projected, qkv_weight, preferred_element_type=jnp.float32
    )
    grad_normed_one, grad_normed_two = (
        lax.psum(grad_normed_one.astype(jnp.bfloat16), "tensor").astype(jnp.float32),
        lax.psum(grad_normed_two.astype(jnp.bfloat16), "tensor").astype(jnp.float32),
    )
    unused_one, norm_back_one = jax.vjp(layer_norm, hidden, norm_rows[0], norm_rows[1])
    unused_two, norm_back_two = jax.vjp(layer_norm, hidden, norm_rows[2], norm_rows[3])
    hidden_one, gain_one, shift_one = norm_back_one(grad_normed_one)
    hidden_two, gain_two, shift_two = norm_back_two(grad_normed_two)
    grad_vectors = jnp.stack([gain_one, shift_one, gain_two, shift_two, grad_bias_sum])
    pieces = (
        grad_qkv_w,
        grad_out_w,
        grad_up_w,
        grad_down_w,
        grad_qkv_bias,
        grad_up_bias,
        grad_vectors,
    )
    return (gradient + hidden_one + hidden_two, pieces)


def stack_member(collected, member):
    return jnp.stack([collected[layer_index][member] for layer_index in range(len(collected))])


def local(
    inputs,
    cotangent,
    qkv_state,
    out_state,
    up_state,
    down_state,
    qkv_bias_state,
    up_bias_state,
    norm_state,
):
    layers = qkv_state.shape[1]
    sequences, row_span, features = inputs.shape
    ctx_place = lax.axis_index("ctx")
    positions = (ctx_place * row_span + jnp.arange(row_span, dtype=jnp.int32)).astype(jnp.float32)
    cosine_table, sine_table = angle_tables(positions, ROT)
    hidden = inputs.astype(jnp.float32)
    fetched = []
    stored = []
    for layer_index in range(layers):
        weights = (
            lax.all_gather(lowered(qkv_state, layer_index), ("dp", "ctx"), axis=0, tiled=True),
            lax.all_gather(lowered(out_state, layer_index), ("dp", "ctx"), axis=1, tiled=True),
            lax.all_gather(lowered(up_state, layer_index), ("dp", "ctx"), axis=0, tiled=True),
            lax.all_gather(lowered(down_state, layer_index), ("dp", "ctx"), axis=1, tiled=True),
            lax.all_gather(lowered(qkv_bias_state, layer_index), ("dp", "ctx"), axis=1, tiled=True),
            lax.all_gather(lowered(up_bias_state, layer_index), ("dp", "ctx"), axis=0, tiled=True),
            lax.all_gather(lowered(norm_state, layer_index), ("dp", "ctx"), axis=1, tiled=True),
        )
        hidden, saved = forward_layer(hidden, weights, cosine_table, sine_table, ctx_place)
        fetched.append(weights)
        stored.append(saved)
    outputs = hidden.astype(jnp.bfloat16)
    gradient = cotangent.astype(jnp.float32)
    collected = [None] * layers
    for layer_index in reversed(range(layers)):
        weights = (
            lax.all_gather(lowered(qkv_state, layer_index), ("dp", "ctx"), axis=0, tiled=True),
            lax.all_gather(lowered(out_state, layer_index), ("dp", "ctx"), axis=1, tiled=True),
            lax.all_gather(lowered(up_state, layer_index), ("dp", "ctx"), axis=0, tiled=True),
            lax.all_gather(lowered(down_state, layer_index), ("dp", "ctx"), axis=1, tiled=True),
            lax.all_gather(lowered(qkv_bias_state, layer_index), ("dp", "ctx"), axis=1, tiled=True),
            lax.all_gather(lowered(up_bias_state, layer_index), ("dp", "ctx"), axis=0, tiled=True),
            lax.all_gather(lowered(norm_state, layer_index), ("dp", "ctx"), axis=1, tiled=True),
        )
        gradient, pieces = backward_layer(
            gradient, weights, stored[layer_index], cosine_table, sine_table, ctx_place
        )
        collected[layer_index] = pieces
    totals = (
        lax.psum_scatter(
            stack_member(collected, 0).astype(jnp.bfloat16),
            ("dp", "ctx"),
            scatter_dimension=1,
            tiled=True,
        ).astype(jnp.float32),
        lax.psum_scatter(
            stack_member(collected, 1).astype(jnp.bfloat16),
            ("dp", "ctx"),
            scatter_dimension=2,
            tiled=True,
        ).astype(jnp.float32),
        lax.psum_scatter(
            stack_member(collected, 2).astype(jnp.bfloat16),
            ("dp", "ctx"),
            scatter_dimension=1,
            tiled=True,
        ).astype(jnp.float32),
        lax.psum_scatter(
            stack_member(collected, 3).astype(jnp.bfloat16),
            ("dp", "ctx"),
            scatter_dimension=2,
            tiled=True,
        ).astype(jnp.float32),
        lax.psum_scatter(
            stack_member(collected, 4).astype(jnp.bfloat16),
            ("dp", "ctx"),
            scatter_dimension=2,
            tiled=True,
        ).astype(jnp.float32),
        lax.psum_scatter(
            stack_member(collected, 5).astype(jnp.bfloat16),
            ("dp", "ctx"),
            scatter_dimension=1,
            tiled=True,
        ).astype(jnp.float32),
        lax.psum_scatter(
            stack_member(collected, 6).astype(jnp.bfloat16),
            ("dp", "ctx"),
            scatter_dimension=2,
            tiled=True,
        ).astype(jnp.float32),
    )
    qkv_pack, qkv_new = adam_step(qkv_state, totals[0], rate_matrix, weight_decay)
    out_pack, out_new = adam_step(out_state, totals[1], rate_matrix, weight_decay)
    up_pack, up_new = adam_step(up_state, totals[2], rate_matrix, weight_decay)
    down_pack, down_new = adam_step(down_state, totals[3], rate_matrix, weight_decay)
    qkv_bias_pack, qkv_bias_new = adam_step(qkv_bias_state, totals[4], rate_vector, 0.0)
    up_bias_pack, up_bias_new = adam_step(up_bias_state, totals[5], rate_vector, 0.0)
    norm_pack, norm_new = adam_step(norm_state, totals[6], rate_vector, 0.0)
    return (
        outputs,
        gradient,
        qkv_pack,
        qkv_new,
        out_pack,
        out_new,
        up_pack,
        up_new,
        down_pack,
        down_new,
        qkv_bias_pack,
        qkv_bias_new,
        up_bias_pack,
        up_bias_new,
        norm_pack,
        norm_new,
    )


def solution(mesh):
    return jax.shard_map(
        local,
        mesh=mesh,
        in_specs=(
            P("dp", "ctx", None),
            P("dp", "ctx", None),
            P(None, None, ("dp", "ctx"), None, "tensor"),
            P(None, None, "tensor", ("dp", "ctx")),
            P(None, None, ("dp", "ctx"), "tensor"),
            P(None, None, "tensor", ("dp", "ctx")),
            P(None, None, None, ("tensor", "dp", "ctx")),
            P(None, None, ("tensor", "dp", "ctx")),
            P(None, None, None, ("dp", "ctx")),
        ),
        out_specs=(
            P("dp", "ctx", None),
            P("dp", "ctx", None),
            P(None, None, ("dp", "ctx"), None, "tensor"),
            P(None, ("dp", "ctx"), None, "tensor"),
            P(None, None, "tensor", ("dp", "ctx")),
            P(None, "tensor", ("dp", "ctx")),
            P(None, None, ("dp", "ctx"), "tensor"),
            P(None, ("dp", "ctx"), "tensor"),
            P(None, None, "tensor", ("dp", "ctx")),
            P(None, "tensor", ("dp", "ctx")),
            P(None, None, None, ("tensor", "dp", "ctx")),
            P(None, None, ("tensor", "dp", "ctx")),
            P(None, None, ("tensor", "dp", "ctx")),
            P(None, ("tensor", "dp", "ctx")),
            P(None, None, None, ("dp", "ctx")),
            P(None, None, ("dp", "ctx")),
        ),
        check_vma=False,
    )
```

profile of v0, /device:TPU:0, one launch (start us, length us, event | category | flops | bytes accessed | tf_op | source)
XLA Modules:
  0.0 2503.2 jit_solution(2617174048600316897)
XLA Ops:
  7.2 7.7 copy.139
  18.0 34.0 %all-gather.2 = bf16[1,1,3,512]{2,1,0,3:T(2,128)(2,1)S(1)} all-gather(bf16[1,1,3,64]{2,1,0,3:T(2,128)(2,1)S(1)} %get-tuple-element.142), channel_id=4, replica_groups=mesh['tensor'=4,'dp'=4,'ctx'=2] {'dp','ctx'}, dimensions={3}, use_global_device_ids=true | all-gather | bytes 3456 | tf_op jit(solution)/shard_map/all_gather | solution.py:284
  52.2 21.0 all-gather
  76.0 46.8 %all-gather.33.cloned.1.call-done = bf16[1,1,2048,3,512]{2,4,3,1,0:T(8,128)(2,1)} async-done(((bf16[1,1,256,3,512]{2,4,3,1,0:T(8,128)(2,1)}), bf16[1,1,2048,3,512]{2,4,3,1,0:T(8,128)(2,1)}) %all-gather.33.cloned.1.call-update) | async-done | bytes 6291472 | tf_op jit(solution)/shard_map/all_gather | solution.py:280
  144.5 8.8 convert.215
  156.5 7.9 convert.217
  170.4 17.8 all-gather.6
  201.0 111.5 %all-gather.39.cloned.1.call-done = bf16[1,1,2048,2048]{3,2,1,0:T(8,128)(2,1)} async-done(((bf16[1,1,256,2048]{3,2,1,0:T(8,128)(2,1)}), bf16[1,1,2048,2048]{3,2,1,0:T(8,128)(2,1)}) %all-gather.39.cloned.1.call-update) | async-done | bytes 8388624 | tf_op jit(solution)/shard_map/all_gather | solution.py:282
  312.5 17.9 multiply_convert_fusion.3
  330.4 107.7 %all-gather.41.cloned.1.call-done = bf16[1,1,2048,2048]{3,2,1,0:T(8,128)(2,1)} async-done(((bf16[1,1,2048,256]{3,2,1,0:T(8,128)(2,1)}), bf16[1,1,2048,2048]{3,2,1,0:T(8,128)(2,1)}) %all-gather.41.cloned.1.call-update) | async-done | bytes 8388624 | tf_op jit(solution)/shard_map/all_gather | solution.py:283
  438.1 10.5 fusion.10
  448.7 39.9 %all-gather.37.cloned.1.call-done = bf16[1,1,512,2048]{3,2,1,0:T(8,128)(2,1)} async-done(((bf16[1,1,512,256]{3,2,1,0:T(8,128)(2,1)}), bf16[1,1,512,2048]{3,2,1,0:T(8,128)(2,1)}) %all-gather.37.cloned.1.call-update) | async-done | bytes 2097168 | tf_op jit(solution)/shard_map/all_gather | solution.py:281
  496.3 30.7 %all-gather.10 = bf16[1,1,3,512]{2,1,0,3:T(2,128)(2,1)S(1)} all-gather(bf16[1,1,3,64]{2,1,0,3:T(2,128)(2,1)S(1)} %get-tuple-element.141), channel_id=12, replica_groups=mesh['tensor'=4,'dp'=4,'ctx'=2] {'dp','ctx'}, dimensions={3}, use_global_device_ids=true | all-gather | bytes 3456 | tf_op jit(solution)/shard_map/all_gather | solution.py:284
  527.2 18.1 all-gather.8
  545.4 33.2 %all-reduce.7.cloned.1.call-done = f32[1,512,2048]{2,1,0:T(8,128)} async-done(((f32[1,512,2048]{2,1,0:T(8,128)}), f32[1,512,2048]{2,1,0:T(8,128)}) %all-reduce.7.cloned.1.call-update) | async-done | bytes 4194320 | tf_op jit(solution)/shard_map/psum | solution.py:130
  583.9 96.9 %all-gather.43.cloned.1.call-done = bf16[1,1,2048,3,512]{2,4,3,1,0:T(8,128)(2,1)} async-done(((bf16[1,1,256,3,512]{2,4,3,1,0:T(8,128)(2,1)}), bf16[1,1,2048,3,512]{2,4,3,1,0:T(8,128)(2,1)}) %all-gather.43.cloned.1.call-update) | async-done | bytes 6291472 | tf_op jit(solution)/shard_map/all_gather | solution.py:280
  680.8 7.1 fusion.145
  700.9 18.2 all-gather.14
  719.1 12.4 all-gather.47.cloned.1.call-done
  735.5 17.5 all-gather.31.cloned.1.call-done
  760.2 119.9 %all-gather.49.cloned.1.call-done = bf16[1,1,2048,2048]{3,2,1,0:T(8,128)(2,1)} async-done(((bf16[1,1,256,2048]{3,2,1,0:T(8,128)(2,1)}), bf16[1,1,2048,2048]{3,2,1,0:T(8,128)(2,1)}) %all-gather.49.cloned.1.call-update) | async-done | bytes 8388624 | tf_op jit(solution)/shard_map/all_gather | solution.py:282
  880.2 19.1 multiply_convert_fusion.2
  909.8 118.3 %all-gather.51.cloned.1.call-done = bf16[1,1,2048,2048]{3,2,1,0:T(8,128)(2,1)} async-done(((bf16[1,1,2048,256]{3,2,1,0:T(8,128)(2,1)}), bf16[1,1,2048,2048]{3,2,1,0:T(8,128)(2,1)}) %all-gather.51.cloned.1.call-update) | async-done | bytes 8388624 | tf_op jit(solution)/shard_map/all_gather | solution.py:283
  1028.1 10.8 fusion.261
  1038.9 9.9 fusion.96
  1051.9 20.0 reduce-scatter.16.cloned.1.call-done
  1075.6 7.5 fusion.104
  1084.8 7.0 fusion.2
  1097.8 71.1 %all-reduce.13.cloned.1.call-done = (bf16[1,512,2048]{2,1,0:T(8,128)(2,1)}, bf16[1,512,2048]{2,1,0:T(8,128)(2,1)}) async-done(((bf16[1,512,2048]{2,1,0:T(8,128)(2,1)}, bf16[1,512,2048]{2,1,0:T(8,128)(2,1)}), (bf16[1,512,2048]{2,1,0:T(8,128)(2,1)}, bf16[1,512,2048]{2,1,0:T(8,128)(2,1)})) %all-reduce.13.cloned.1.call-update) | async-done | bytes 4194320 | tf_op jit(solution)/shard_map/psum | solution.py:236
  1178.6 78.8 %all-reduce.9.cloned.1.call-done = f32[1,512,2048]{2,1,0:T(8,128)} async-done(((f32[1,512,2048]{2,1,0:T(8,128)}), f32[1,512,2048]{2,1,0:T(8,128)}) %all-reduce.9.cloned.1.call-update) | async-done | bytes 4194320 | tf_op jit(solution)/shard_map/psum | solution.py:130
  1257.3 7.6 fusion.241
  1283.9 12.3 fusion.262
  1297.5 9.3 fusion.99
  1308.8 8.1 reduce-scatter.20.cloned.1.call-done
  1330.8 8.0 fusion.107
  1356.5 68.0 %all-reduce.11.cloned.1.call-done = (bf16[1,512,2048]{2,1,0:T(8,128)(2,1)}, bf16[1,512,2048]{2,1,0:T(8,128)(2,1)}) async-done(((bf16[1,512,2048]{2,1,0:T(8,128)(2,1)}, bf16[1,512,2048]{2,1,0:T(8,128)(2,1)}), (bf16[1,512,2048]{2,1,0:T(8,128)(2,1)}, bf16[1,512,2048]{2,1,0:T(8,128)(2,1)})) %all-reduce.11.cloned.1.call-update) | async-done | bytes 4194320 | tf_op jit(solution)/shard_map/psum | solution.py:235
  1460.8 7.8 convert_bitcast_fusion.2
  1480.7 6.9 convert_bitcast_fusion
  1492.6 6.7 pad_maximum_fusion.1
  1502.3 52.5 %reduce-scatter.34.cloned.1.call-done = bf16[64,6]{1,0:T(8,128)(2,1)} async-done(((bf16[512,6]{1,0:T(8,128)(2,1)}), bf16[64,6]{1,0:T(8,128)(2,1)}) %reduce-scatter.34.cloned.1.call-update) | async-done | bytes 784
  1563.4 48.9 %reduce-scatter.32.cloned.1.call-done = bf16[2,5,256]{2,1,0:T(8,128)(2,1)} async-done(((bf16[2,5,2048]{2,1,0:T(8,128)(2,1)}), bf16[2,5,256]{2,1,0:T(8,128)(2,1)}) %reduce-scatter.32.cloned.1.call-update) | async-done | bytes 5136 | tf_op jit(solution)/shard_map/reduce_scatter | solution.py:345
  1615.0 89.1 %reduce-scatter.26.cloned.1.call-done = bf16[2,512,256]{2,1,0:T(8,128)(2,1)} async-done(((bf16[2,512,2048]{2,1,0:T(8,128)(2,1)}), bf16[2,512,256]{2,1,0:T(8,128)(2,1)}) %reduce-scatter.26.cloned.1.call-update) | async-done | bytes 524304 | tf_op jit(solution)/shard_map/reduce_scatter | solution.py:315
  1710.9 204.9 %reduce-scatter.24.cloned.1.call-done = bf16[2,256,3,512]{3,1,2,0:T(8,128)(2,1)} async-done(((bf16[2,2048,3,512]{3,1,2,0:T(8,128)(2,1)}), bf16[2,256,3,512]{3,1,2,0:T(8,128)(2,1)}) %reduce-scatter.24.cloned.1.call-update) | async-done | bytes 1572880 | tf_op jit(solution)/shard_map/reduce_scatter | solution.py:309
  1928.8 269.4 %reduce-scatter.28.cloned.1.call-done = bf16[2,256,2048]{2,1,0:T(8,128)(2,1)} async-done(((bf16[2,2048,2048]{2,1,0:T(8,128)(2,1)}), bf16[2,256,2048]{2,1,0:T(8,128)(2,1)}) %reduce-scatter.28.cloned.1.call-update) | async-done | bytes 2097168 | tf_op jit(solution)/shard_map/reduce_scatter | solution.py:321
  2200.5 9.1 fusion.63
  2209.6 10.1 pad_maximum_fusion.3
  2219.6 261.5 %reduce-scatter.30.cloned.1.call-done = bf16[2,2048,256]{2,1,0:T(8,128)(2,1)} async-done(((bf16[2,2048,2048]{2,1,0:T(8,128)(2,1)}), bf16[2,2048,256]{2,1,0:T(8,128)(2,1)}) %reduce-scatter.30.cloned.1.call-update) | async-done | bytes 2097168 | tf_op jit(solution)/shard_map/reduce_scatter | solution.py:327
  2481.1 9.6 fusion.62
  (411 shorter events, 269.0 us)
Async XLA Ops:
  7.2 10.6 copy-start.61
  7.2 10.6 copy-start.65
  7.2 115.6 %all-gather.33.cloned.1.call-start = ((), (), s32[]{:S(2)}) async-start(), calls=%async_computation.24 | async-start | bytes 7077888 | tf_op jit(solution)/shard_map/all_gather | solution.py:280
  14.9 58.4 %copy-start.2 = (bf16[1,512,2048]{2,1,0:T(8,128)(2,1)S(1)}, bf16[1,512,2048]{2,1,0:T(8,128)(2,1)}, u32[]{:S(2)}) copy-start(bf16[1,512,2048]{2,1,0:T(8,128)(2,1)} %param.9) | copy-start | bytes 6291460
  17.7 173.2 %all-gather.29.cloned.1.call-start = ((), (), s32[]{:S(2)}) async-start(), calls=%async_computation.11 | async-start | bytes 1572864 | tf_op jit(solution)/shard_map/all_gather | solution.py:106
  73.6 238.9 %copy-start.63 = (f32[512]{0:T(512)}, f32[512]{0:T(512)S(1)}, u32[]{:S(2)}) copy-start(f32[512]{0:T(512)S(1)} %broadcast_multiply_fusion.1) | copy-start | bytes 6148
  74.9 237.6 %copy-start.69 = (f32[512]{0:T(512)}, f32[512]{0:T(512)S(1)}, u32[]{:S(2)}) copy-start(f32[512]{0:T(512)S(1)} %fusion.221) | copy-start | bytes 6148
  75.9 52.7 %copy-start.57 = (f32[1,1,1,2048]{3,1,2,0:T(1,128)}, f32[1,1,1,2048]{3,1,2,0:T(1,128)S(1)}, u32[]{:S(2)}) copy-start(f32[1,1,1,2048]{3,1,2,0:T(1,128)S(1)} %get-tuple-element.148) | copy-start | bytes 24580
  76.0 52.7 %copy-start.79 = (f32[1,1,1,2048]{3,1,2,0:T(1,128)}, f32[1,1,1,2048]{3,1,2,0:T(1,128)S(1)}, u32[]{:S(2)}) copy-start(f32[1,1,1,2048]{3,1,2,0:T(1,128)S(1)} %get-tuple-element.149) | copy-start | bytes 24580
  76.0 236.6 %copy-start.59 = (f32[1,1,1,2048]{3,1,2,0:T(1,128)}, f32[1,1,1,2048]{3,1,2,0:T(1,128)S(1)}, u32[]{:S(2)}) copy-start(f32[1,1,1,2048]{3,1,2,0:T(1,128)S(1)} %get-tuple-element.150) | copy-start | bytes 24580
  76.0 236.5 %copy-start.77 = (f32[1,1,1,2048]{3,1,2,0:T(1,128)}, f32[1,1,1,2048]{3,1,2,0:T(1,128)S(1)}, u32[]{:S(2)}) copy-start(f32[1,1,1,2048]{3,1,2,0:T(1,128)S(1)} %get-tuple-element.151) | copy-start | bytes 24580
  141.0 49.9 %copy-start.53 = (bf16[512,2,32]{2,0,1:T(8,128)(2,1)}, bf16[512,2,32]{2,0,1:T(8,128)(2,1)S(1)}, u32[]{:S(2)}) copy-start(bf16[512,2,32]{2,0,1:T(8,128)(2,1)S(1)} %get-tuple-element.129) | copy-start | bytes 196612
  142.3 54.8 %all-gather.35.cloned.1.call-start = ((), (), s32[]{:S(2)}) async-start(), calls=%async_computation.25 | async-start | bytes 1572864 | tf_op jit(solution)/shard_map/all_gather | solution.py:107
  144.5 168.1 %all-gather.39.cloned.1.call-start = ((), (), s32[]{:S(2)}) async-start(), calls=%async_computation.27 | async-start | bytes 9437184 | tf_op jit(solution)/shard_map/all_gather | solution.py:282
  156.4 281.7 %all-gather.41.cloned.1.call-start = ((), (), s32[]{:S(2)}) async-start(), calls=%async_computation.28 | async-start | bytes 9437184 | tf_op jit(solution)/shard_map/all_gather | solution.py:283
  167.4 321.2 %all-gather.37.cloned.1.call-start = ((), (), s32[]{:S(2)}) async-start(), calls=%async_computation.26 | async-start | bytes 2359296 | tf_op jit(solution)/shard_map/all_gather | solution.py:281
  170.3 408.2 %all-reduce.7.cloned.1.call-start = ((), (), s32[]{:S(2)}) async-start(), calls=%async_computation.12 | async-start | bytes 8388608 | tf_op jit(solution)/shard_map/psum | solution.py:130
  188.3 124.3 %copy-start.85 = (f32[1,1,2048]{2,1,0:T(1,128)}, f32[1,1,2048]{2,1,0:T(1,128)S(1)}, u32[]{:S(2)}) copy-start(f32[1,1,2048]{2,1,0:T(1,128)S(1)} %convert_element_type.508) | copy-start | bytes 24580
  201.0 287.6 %copy-start.37 = (bf16[2,256,512]{2,1,0:T(8,128)(2,1)}, bf16[2,256,512]{2,1,0:T(8,128)(2,1)S(1)}, u32[]{:S(2)}) copy-start(bf16[2,256,512]{2,1,0:T(8,128)(2,1)S(1)} %fusion.177) | copy-start | bytes 1572868
  494.7 186.1 %all-gather.43.cloned.1.call-start = ((), (), s32[]{:S(2)}) async-start(), calls=%async_computation.29 | async-start | bytes 7077888 | tf_op jit(solution)/shard_map/all_gather | solution.py:280
  495.5 236.0 %all-gather.47.cloned.1.call-start = ((), (), s32[]{:S(2)}) async-start(), calls=%async_computation.31 | async-start | bytes 2359296 | tf_op jit(solution)/shard_map/all_gather | solution.py:281
  496.2 256.7 %all-gather.31.cloned.1.call-start = ((), (), s32[]{:S(2)}) async-start(), calls=%async_computation.13 | async-start | bytes 1572864 | tf_op jit(solution)/shard_map/all_gather | solution.py:106
  545.3 135.5 %copy-start.83 = (f32[1,1,1,2048]{3,1,2,0:T(1,128)}, f32[1,1,1,2048]{3,1,2,0:T(1,128)S(1)}, u32[]{:S(2)}) copy-start(f32[1,1,1,2048]{3,1,2,0:T(1,128)S(1)} %get-tuple-element.145) | copy-start | bytes 24580
  545.3 334.8 %copy-start.81 = (f32[1,1,1,2048]{3,1,2,0:T(1,128)}, f32[1,1,1,2048]{3,1,2,0:T(1,128)S(1)}, u32[]{:S(2)}) copy-start(f32[1,1,1,2048]{3,1,2,0:T(1,128)S(1)} %get-tuple-element.147) | copy-start | bytes 24580
  693.1 38.4 %copy-start.13 = (bf16[1,512,2048]{2,1,0:T(8,128)(2,1)S(1)}, bf16[1,512,2048]{2,1,0:T(8,128)(2,1)}, u32[]{:S(2)}) copy-start(bf16[1,512,2048]{2,1,0:T(8,128)(2,1)} %param.10) | copy-start | bytes 6291460
  697.2 183.0 %all-gather.49.cloned.1.call-start = ((), (), s32[]{:S(2)}) async-start(), calls=%async_computation.32 | async-start | bytes 9437184 | tf_op jit(solution)/shard_map/all_gather | solution.py:282
  697.9 203.2 %all-gather.45.cloned.1.call-start = ((), (), s32[]{:S(2)}) async-start(), calls=%async_computation.30 | async-start | bytes 1572864 | tf_op jit(solution)/shard_map/all_gather | solution.py:107
  700.1 328.0 %all-gather.51.cloned.1.call-start = ((), (), s32[]{:S(2)}) async-start(), calls=%async_computation.33 | async-start | bytes 9437184 | tf_op jit(solution)/shard_map/all_gather | solution.py:283
  700.8 349.0 %reduce-scatter.18.cloned.1.call-start = ((), (), s32[]{:S(2)}) async-start(), calls=%async_computation.16 | async-start | bytes 1572864 | tf_op jit(solution)/shard_map/reduce_scatter | solution.py:212
  759.8 312.1 %reduce-scatter.16.cloned.1.call-start = ((), (), s32[]{:S(2)}) async-start(), calls=%async_computation.15 | async-start | bytes 1572864 | tf_op jit(solution)/shard_map/reduce_scatter | solution.py:209
  909.5 259.3 %all-reduce.13.cloned.1.call-start = ((), (), s32[]{:S(2)}) async-start(), calls=%async_computation.37 | async-start | bytes 8388608 | tf_op jit(solution)/shard_map/psum | solution.py:236
  1038.9 10.0 copy-start.89
  1083.2 174.1 %all-reduce.9.cloned.1.call-start = ((), (), s32[]{:S(2)}) async-start(), calls=%async_computation.14 | async-start | bytes 8388608 | tf_op jit(solution)/shard_map/psum | solution.py:130
  1097.1 209.6 %reduce-scatter.22.cloned.1.call-start = ((), (), s32[]{:S(2)}) async-start(), calls=%async_computation.18 | async-start | bytes 1572864 | tf_op jit(solution)/shard_map/reduce_scatter | solution.py:212
  1273.0 43.9 %reduce-scatter.20.cloned.1.call-start = ((), (), s32[]{:S(2)}) async-start(), calls=%async_computation.17 | async-start | bytes 1572864 | tf_op jit(solution)/shard_map/reduce_scatter | solution.py:209
  1283.8 140.7 %all-reduce.11.cloned.1.call-start = ((), (), s32[]{:S(2)}) async-start(), calls=%async_computation.36 | async-start | bytes 8388608 | tf_op jit(solution)/shard_map/psum | solution.py:235
  1323.3 15.5 copy-start.24
  1338.8 161.3 %reduce-scatter.36.cloned.1.call-start = ((), (), s32[]{:S(2)}) async-start(), calls=%async_computation.35 | async-start | bytes 589824
  1353.5 72.9 %copy-start.3 = (bf16[1,512,2048]{2,1,0:T(8,128)(2,1)S(1)}, bf16[1,512,2048]{2,1,0:T(8,128)(2,1)}, u32[]{:S(2)}) copy-start(bf16[1,512,2048]{2,1,0:T(8,128)(2,1)} %param.9) | copy-start | bytes 6291460
  1353.5 72.9 %copy-start.58 = (f32[1,1,1,2048]{3,1,2,0:T(1,128)S(1)}, f32[1,1,1,2048]{3,1,2,0:T(1,128)}, u32[]{:S(2)}) copy-start(f32[1,1,1,2048]{3,1,2,0:T(1,128)} %copy-done.57) | copy-start | bytes 24580
  1353.5 72.9 %copy-start.60 = (f32[1,1,1,2048]{3,1,2,0:T(1,128)S(1)}, f32[1,1,1,2048]{3,1,2,0:T(1,128)}, u32[]{:S(2)}) copy-start(f32[1,1,1,2048]{3,1,2,0:T(1,128)} %copy-done.59) | copy-start | bytes 24580
  1353.5 72.9 %copy-start.64 = (f32[512]{0:T(512)S(1)}, f32[512]{0:T(512)}, u32[]{:S(2)}) copy-start(f32[512]{0:T(512)} %copy-done.63) | copy-start | bytes 6148
  1353.6 201.2 %reduce-scatter.34.cloned.1.call-start = ((), (), s32[]{:S(2)}) async-start(), calls=%async_computation.34 | async-start | bytes 147456
  1356.2 256.1 %reduce-scatter.32.cloned.1.call-start = ((), (), s32[]{:S(2)}) async-start(), calls=%async_computation.23 | async-start | bytes 73728 | tf_op jit(solution)/shard_map/reduce_scatter | solution.py:345
  1438.4 265.8 %reduce-scatter.26.cloned.1.call-start = ((), (), s32[]{:S(2)}) async-start(), calls=%async_computation.20 | async-start | bytes 4718592 | tf_op jit(solution)/shard_map/reduce_scatter | solution.py:315
  1443.1 472.8 %reduce-scatter.24.cloned.1.call-start = ((), (), s32[]{:S(2)}) async-start(), calls=%async_computation.19 | async-start | bytes 14155776 | tf_op jit(solution)/shard_map/reduce_scatter | solution.py:309
  1460.1 738.1 %reduce-scatter.28.cloned.1.call-start = ((), (), s32[]{:S(2)}) async-start(), calls=%async_computation.21 | async-start | bytes 18874368 | tf_op jit(solution)/shard_map/reduce_scatter | solution.py:321
  1480.6 1000.5 %reduce-scatter.30.cloned.1.call-start = ((), (), s32[]{:S(2)}) async-start(), calls=%async_computation.22 | async-start | bytes 18874368 | tf_op jit(solution)/shard_map/reduce_scatter | solution.py:327
  (71 other events, 270.3 us)
Sparse Core Ops, SparseCore 0:
  17.8 104.9 all-gather.32
  142.4 19.4 all-gather.28
  164.0 21.3 all-gather.34
  188.0 124.4 all-gather.38
  315.0 123.1 all-gather.40
  440.0 48.4 all-gather.36
  494.8 83.6 all-reduce.6
  581.2 99.6 all-gather.42
  682.9 48.5 all-gather.46
  733.5 19.4 all-gather.30
  755.7 124.4 all-gather.48
  881.6 19.4 all-gather.44
  903.1 124.9 all-gather.50
  1030.2 18.5 reduce-scatter.17
  1051.4 20.3 reduce-scatter.15
  1083.4 85.4 all-reduce.12
  1171.7 85.6 all-reduce.8
  1273.1 20.5 reduce-scatter.21
  1296.5 20.3 reduce-scatter.19
  1338.9 85.4 all-reduce.10
  1427.8 62.7 reduce-scatter.35
  1493.9 60.8 reduce-scatter.33
  1558.5 53.7 reduce-scatter.31
  1616.4 87.7 reduce-scatter.25
  1708.3 207.4 reduce-scatter.23
  1919.5 278.6 reduce-scatter.27
  2201.8 279.2 reduce-scatter.29
where the time goes:
time: 2510 us; the launch traced here: 2500 us
  waiting for transfers between devices  1880 us (75%)
  matrix products  212 us (8%)
  other arithmetic  172 us (7%)
  blocking collectives  140 us (6%)
  local copies, waits for them, and re-layouts  78.9 us (3%)
    reduce_scatter x1, waiting for transfers between devices, local(): lax.psum_scatter(stack_member(collected, 2).astype(jnp.bfloat16), ('dp',...  269 us
    reduce_scatter x1, waiting for transfers between devices, local(): lax.psum_scatter(stack_member(collected, 3).astype(jnp.bfloat16), ('dp',...  261 us
    all_gather x2, waiting for transfers between devices, local(): lax.all_gather(lowered(up_state, layer_index), ('dp', 'ctx'), axis=0, til...  231 us
    all_gather x2, waiting for transfers between devices, local(): lax.all_gather(lowered(down_state, layer_index), ('dp', 'ctx'), axis=1, t...  226 us
    reduce_scatter x1, waiting for transfers between devices, local(): lax.psum_scatter(stack_member(collected, 0).astype(jnp.bfloat16), ('dp',...  205 us
    all_gather x2, waiting for transfers between devices, local(): lax.all_gather(lowered(qkv_state, layer_index), ('dp', 'ctx'), axis=0, ti...  144 us
    psum x2, waiting for transfers between devices, forward_layer(): branch = lax.psum(summand, 'tensor')  112 us
    reduce_scatter x1, waiting for transfers between devices, local(): lax.psum_scatter(stack_member(collected, 1).astype(jnp.bfloat16), ('dp',...  89.1 us
  transfers between devices with their start and end apart: 27, of which 22 were waited for; matrix products, arithmetic and copies ran while one was open for 14% of the time, Pallas kernels for 0%

commit v1 on v0

--- a/solution.py
+++ b/solution.py
@@ -1,3 +1,4 @@
+import functools
 import jax
 import jax.numpy as jnp
 from jax import lax
@@ -13,6 +14,21 @@
 rate_matrix = 0.008
 rate_vector = 0.2
 weight_decay = 0.01
+
+
+def divide_sample_on_mesh(my_tile, mesh_name):
+    n_blocks = lax.axis_size(mesh_name)
+    t_next, mixed_arr = (my_tile, 0)
+    while 1 << mixed_arr < n_blocks:
+        tile_out = lax.ppermute(
+            t_next, mesh_name, list(map(lambda rr: (rr, rr ^ 1 << mixed_arr), range(n_blocks)))
+        )
+        t_next = t_next + tile_out
+        mixed_arr = mixed_arr + 1
+    return t_next
+
+
+draw_signs_over_axis = functools.partial(divide_sample_on_mesh, mesh_name="tensor")
 
 
 def layer_norm(values, norm_gain, norm_shift):
@@ -127,7 +143,7 @@
     summand = summand + jnp.einsum(
         "scf,fd->scd", activation, down_weight, preferred_element_type=jnp.float32
     )
-    branch = lax.psum(summand, "tensor")
+    branch = draw_signs_over_axis(summand)
     saved = (
         hidden,
         normed_one,

time: 2510 us -> 2420 us (0.964)
  waiting for transfers between devices: 1880 us -> 1760 us
    psum x2 -> x0, waiting for transfers between devices: 112 us -> none  [forward_layer(): branch = lax.psum(summand, 'tensor')]
    all_gather x2, waiting for transfers between devices: 144 us -> 46.8 us  [local(): lax.all_gather(lowered(qkv_state, layer_index), ('dp', 'ctx'), axis=0, ti...]
    psum x1, waiting for transfers between devices: 71.1 us -> 151 us  [backward_layer(): lax.psum(grad_normed_two.astype(jnp.bfloat16), 'tensor').astype(jnp.float32)]
    ppermute x0 -> x4, waiting for transfers between devices: none -> 37.8 us  [divide_sample_on_mesh(): lax.ppermute(t_next, mesh_name, list(map(lambda rr: (rr, rr ^ 1 << mixed_...]
    unnamed x29 -> x27, waiting for transfers between devices: 55.6 us -> 55.1 us
  transfers between devices with their start and end apart: 27 -> 29, of which waited for: 22 -> 21; matrix products, arithmetic and copies ran while one was open for 14% -> 16% of each run, Pallas kernels for 0% -> 0%
where the time goes in v1:
time: 2420 us; the launch traced here: 2410 us
  waiting for transfers between devices  1760 us (73%)
  matrix products  215 us (9%)
  other arithmetic  182 us (8%)
  blocking collectives  152 us (6%)
  local copies, waits for them, and re-layouts  81 us (3%)
    reduce_scatter x1, waiting for transfers between devices, local(): lax.psum_scatter(stack_member(collected, 2).astype(jnp.bfloat16), ('dp',...  269 us
    reduce_scatter x1, waiting for transfers between devices, local(): lax.psum_scatter(stack_member(collected, 3).astype(jnp.bfloat16), ('dp',...  262 us
    all_gather x2, waiting for transfers between devices, local(): lax.all_gather(lowered(up_state, layer_index), ('dp', 'ctx'), axis=0, til...  227 us
    all_gather x2, waiting for transfers between devices, local(): lax.all_gather(lowered(down_state, layer_index), ('dp', 'ctx'), axis=1, t...  213 us
    reduce_scatter x1, waiting for transfers between devices, local(): lax.psum_scatter(stack_member(collected, 0).astype(jnp.bfloat16), ('dp',...  205 us
    psum x1, waiting for transfers between devices, backward_layer(): lax.psum(grad_normed_two.astype(jnp.bfloat16), 'tensor').astype(jnp.float32)  151 us
    reduce_scatter x1, waiting for transfers between devices, local(): lax.psum_scatter(stack_member(collected, 1).astype(jnp.bfloat16), ('dp',...  89.3 us
    psum x1, waiting for transfers between devices, backward_layer(): lax.psum(grad_normed_one.astype(jnp.bfloat16), 'tensor').astype(jnp.float32)  68 us
  transfers between devices with their start and end apart: 29, of which 21 were waited for; matrix products, arithmetic and copies ran while one was open for 16% of the time, Pallas kernels for 0%

profile of v1, /device:TPU:0, one launch (start us, length us, event | category | flops | bytes accessed | tf_op | source)
XLA Modules:
  0.0 2410.4 jit_solution(14158617863019300396)
XLA Ops:
  7.2 7.7 copy.139
  18.0 34.0 %all-gather.2 = bf16[1,1,3,512]{2,1,0,3:T(2,128)(2,1)S(1)} all-gather(bf16[1,1,3,64]{2,1,0,3:T(2,128)(2,1)S(1)} %get-tuple-element.142), channel_id=4, replica_groups=mesh['tensor'=4,'dp'=4,'ctx'=2] {'dp','ctx'}, dimensions={3}, use_global_device_ids=true | all-gather | bytes 3456 | tf_op jit(solution)/shard_map/all_gather | solution.py:300
  52.2 21.0 all-gather
  76.0 46.8 %all-gather.33.cloned.1.call-done = bf16[1,1,2048,3,512]{2,4,3,1,0:T(8,128)(2,1)} async-done(((bf16[1,1,256,3,512]{2,4,3,1,0:T(8,128)(2,1)}), bf16[1,1,2048,3,512]{2,4,3,1,0:T(8,128)(2,1)}) %all-gather.33.cloned.1.call-update) | async-done | bytes 6291472 | tf_op jit(solution)/shard_map/all_gather | solution.py:296
  144.5 8.8 convert.215
  156.5 7.9 convert.217
  173.3 18.0 all-gather.6
  203.9 108.7 %all-gather.39.cloned.1.call-done = bf16[1,1,2048,2048]{3,2,1,0:T(8,128)(2,1)} async-done(((bf16[1,1,256,2048]{3,2,1,0:T(8,128)(2,1)}), bf16[1,1,2048,2048]{3,2,1,0:T(8,128)(2,1)}) %all-gather.39.cloned.1.call-update) | async-done | bytes 8388624 | tf_op jit(solution)/shard_map/all_gather | solution.py:298
  312.6 17.9 multiply_convert_fusion.3
  330.4 107.7 %all-gather.41.cloned.1.call-done = bf16[1,1,2048,2048]{3,2,1,0:T(8,128)(2,1)} async-done(((bf16[1,1,2048,256]{3,2,1,0:T(8,128)(2,1)}), bf16[1,1,2048,2048]{3,2,1,0:T(8,128)(2,1)}) %all-gather.41.cloned.1.call-update) | async-done | bytes 8388624 | tf_op jit(solution)/shard_map/all_gather | solution.py:299
  438.2 10.5 fusion.10
  448.7 40.5 %all-gather.37.cloned.1.call-done = bf16[1,1,512,2048]{3,2,1,0:T(8,128)(2,1)} async-done(((bf16[1,1,512,256]{3,2,1,0:T(8,128)(2,1)}), bf16[1,1,512,2048]{3,2,1,0:T(8,128)(2,1)}) %all-gather.37.cloned.1.call-update) | async-done | bytes 2097168 | tf_op jit(solution)/shard_map/all_gather | solution.py:297
  493.5 7.1 collective-permute-done
  504.9 32.1 %all-gather.10 = bf16[1,1,3,512]{2,1,0,3:T(2,128)(2,1)S(1)} all-gather(bf16[1,1,3,64]{2,1,0,3:T(2,128)(2,1)S(1)} %get-tuple-element.141), channel_id=12, replica_groups=mesh['tensor'=4,'dp'=4,'ctx'=2] {'dp','ctx'}, dimensions={3}, use_global_device_ids=true | all-gather | bytes 3456 | tf_op jit(solution)/shard_map/all_gather | solution.py:300
  537.1 28.5 %all-gather.8 = bf16[1,1,5,2048]{3,1,2,0:T(2,128)(2,1)S(1)} all-gather(bf16[1,1,5,256]{3,1,2,0:T(2,128)(2,1)S(1)} %get-tuple-element.159), channel_id=10, replica_groups=mesh['tensor'=4,'dp'=4,'ctx'=2] {'dp','ctx'}, dimensions={3}, use_global_device_ids=true | all-gather | bytes 23040 | tf_op jit(solution)/shard_map/all_gather | solution.py:302
  565.7 30.7 %collective-permute-done.1 = f32[1,512,2048]{2,1,0:T(8,128)} collective-permute-done((f32[1,512,2048]{2,1,0:T(8,128)}, f32[1,512,2048]{2,1,0:T(8,128)}, u32[]{:S(2)}, u32[]{:S(2)}) %collective-permute-start.1) | collective-permute-done | bytes 4194336 | tf_op jit(solution)/shard_map/ppermute | solution.py:23
  603.2 7.2 fusion.145
  620.6 18.4 all-gather.14
  650.9 118.1 %all-gather.49.cloned.1.call-done = bf16[1,1,2048,2048]{3,2,1,0:T(8,128)(2,1)} async-done(((bf16[1,1,256,2048]{3,2,1,0:T(8,128)(2,1)}), bf16[1,1,2048,2048]{3,2,1,0:T(8,128)(2,1)}) %all-gather.49.cloned.1.call-update) | async-done | bytes 8388624 | tf_op jit(solution)/shard_map/all_gather | solution.py:298
  769.0 19.3 multiply_convert_fusion.2
  788.3 105.7 %all-gather.51.cloned.1.call-done = bf16[1,1,2048,2048]{3,2,1,0:T(8,128)(2,1)} async-done(((bf16[1,1,2048,256]{3,2,1,0:T(8,128)(2,1)}), bf16[1,1,2048,2048]{3,2,1,0:T(8,128)(2,1)}) %all-gather.51.cloned.1.call-update) | async-done | bytes 8388624 | tf_op jit(solution)/shard_map/all_gather | solution.py:299
  894.0 10.5 fusion.2
  904.5 11.2 all-gather.31.cloned.1.call-done
  922.5 15.8 all-gather.45.cloned.1.call-done
  952.1 11.4 fusion.261
  963.5 9.9 fusion.96
  976.5 7.6 reduce-scatter.16.cloned.1.call-done
  988.8 6.8 add.385
  997.1 7.4 fusion.104
  1005.1 150.6 %all-reduce.7.cloned.1.call-done = (bf16[1,512,2048]{2,1,0:T(8,128)(2,1)}, bf16[1,512,2048]{2,1,0:T(8,128)(2,1)}) async-done(((bf16[1,512,2048]{2,1,0:T(8,128)(2,1)}, bf16[1,512,2048]{2,1,0:T(8,128)(2,1)}), (bf16[1,512,2048]{2,1,0:T(8,128)(2,1)}, bf16[1,512,2048]{2,1,0:T(8,128)(2,1)})) %all-reduce.7.cloned.1.call-update) | async-done | bytes 4194320 | tf_op jit(solution)/shard_map/psum | solution.py:252
  1165.4 7.3 fusion.241
  1191.2 12.5 fusion.262
  1205.0 9.5 fusion.99
  1216.5 7.8 reduce-scatter.20.cloned.1.call-done
  1238.2 8.0 fusion.107
  1263.9 68.0 %all-reduce.5.cloned.1.call-done = (bf16[1,512,2048]{2,1,0:T(8,128)(2,1)}, bf16[1,512,2048]{2,1,0:T(8,128)(2,1)}) async-done(((bf16[1,512,2048]{2,1,0:T(8,128)(2,1)}, bf16[1,512,2048]{2,1,0:T(8,128)(2,1)}), (bf16[1,512,2048]{2,1,0:T(8,128)(2,1)}, bf16[1,512,2048]{2,1,0:T(8,128)(2,1)})) %all-reduce.5.cloned.1.call-update) | async-done | bytes 4194320 | tf_op jit(solution)/shard_map/psum | solution.py:251
  1368.2 7.8 convert_bitcast_fusion.2
  1388.1 6.9 convert_bitcast_fusion
  1400.3 6.8 pad_maximum_fusion.1
  1410.0 52.1 %reduce-scatter.34.cloned.1.call-done = bf16[64,6]{1,0:T(8,128)(2,1)} async-done(((bf16[512,6]{1,0:T(8,128)(2,1)}), bf16[64,6]{1,0:T(8,128)(2,1)}) %reduce-scatter.34.cloned.1.call-update) | async-done | bytes 784
  1470.7 48.9 %reduce-scatter.32.cloned.1.call-done = bf16[2,5,256]{2,1,0:T(8,128)(2,1)} async-done(((bf16[2,5,2048]{2,1,0:T(8,128)(2,1)}), bf16[2,5,256]{2,1,0:T(8,128)(2,1)}) %reduce-scatter.32.cloned.1.call-update) | async-done | bytes 5136 | tf_op jit(solution)/shard_map/reduce_scatter | solution.py:361
  1522.3 89.3 %reduce-scatter.26.cloned.1.call-done = bf16[2,512,256]{2,1,0:T(8,128)(2,1)} async-done(((bf16[2,512,2048]{2,1,0:T(8,128)(2,1)}), bf16[2,512,256]{2,1,0:T(8,128)(2,1)}) %reduce-scatter.26.cloned.1.call-update) | async-done | bytes 524304 | tf_op jit(solution)/shard_map/reduce_scatter | solution.py:331
  1618.4 204.9 %reduce-scatter.24.cloned.1.call-done = bf16[2,256,3,512]{3,1,2,0:T(8,128)(2,1)} async-done(((bf16[2,2048,3,512]{3,1,2,0:T(8,128)(2,1)}), bf16[2,256,3,512]{3,1,2,0:T(8,128)(2,1)}) %reduce-scatter.24.cloned.1.call-update) | async-done | bytes 1572880 | tf_op jit(solution)/shard_map/reduce_scatter | solution.py:325
  1836.2 269.4 %reduce-scatter.28.cloned.1.call-done = bf16[2,256,2048]{2,1,0:T(8,128)(2,1)} async-done(((bf16[2,2048,2048]{2,1,0:T(8,128)(2,1)}), bf16[2,256,2048]{2,1,0:T(8,128)(2,1)}) %reduce-scatter.28.cloned.1.call-update) | async-done | bytes 2097168 | tf_op jit(solution)/shard_map/reduce_scatter | solution.py:337
  2107.9 9.1 fusion.63
  2117.0 10.1 pad_maximum_fusion.3
  2127.1 261.6 %reduce-scatter.30.cloned.1.call-done = bf16[2,2048,256]{2,1,0:T(8,128)(2,1)} async-done(((bf16[2,2048,2048]{2,1,0:T(8,128)(2,1)}), bf16[2,2048,256]{2,1,0:T(8,128)(2,1)}) %reduce-scatter.30.cloned.1.call-update) | async-done | bytes 2097168 | tf_op jit(solution)/shard_map/reduce_scatter | solution.py:343
  2388.7 9.6 fusion.62
  (411 shorter events, 277.6 us)
Async XLA Ops:
  7.2 10.6 copy-start.64
  7.2 115.6 %all-gather.33.cloned.1.call-start = ((), (), s32[]{:S(2)}) async-start(), calls=%async_computation.22 | async-start | bytes 7077888 | tf_op jit(solution)/shard_map/all_gather | solution.py:296
  14.9 58.4 %copy-start.2 = (bf16[1,512,2048]{2,1,0:T(8,128)(2,1)S(1)}, bf16[1,512,2048]{2,1,0:T(8,128)(2,1)}, u32[]{:S(2)}) copy-start(bf16[1,512,2048]{2,1,0:T(8,128)(2,1)} %param.9) | copy-start | bytes 6291460
  17.7 176.3 %all-gather.29.cloned.1.call-start = ((), (), s32[]{:S(2)}) async-start(), calls=%async_computation.11 | async-start | bytes 1572864 | tf_op jit(solution)/shard_map/all_gather | solution.py:122
  73.6 238.9 %copy-start.62 = (f32[512]{0:T(512)}, f32[512]{0:T(512)S(1)}, u32[]{:S(2)}) copy-start(f32[512]{0:T(512)S(1)} %broadcast_multiply_fusion.1) | copy-start | bytes 6148
  74.9 237.7 %copy-start.68 = (f32[512]{0:T(512)}, f32[512]{0:T(512)S(1)}, u32[]{:S(2)}) copy-start(f32[512]{0:T(512)S(1)} %fusion.221) | copy-start | bytes 6148
  75.9 52.7 %copy-start.56 = (f32[1,1,1,2048]{3,1,2,0:T(1,128)}, f32[1,1,1,2048]{3,1,2,0:T(1,128)S(1)}, u32[]{:S(2)}) copy-start(f32[1,1,1,2048]{3,1,2,0:T(1,128)S(1)} %get-tuple-element.148) | copy-start | bytes 24580
  76.0 52.7 %copy-start.78 = (f32[1,1,1,2048]{3,1,2,0:T(1,128)}, f32[1,1,1,2048]{3,1,2,0:T(1,128)S(1)}, u32[]{:S(2)}) copy-start(f32[1,1,1,2048]{3,1,2,0:T(1,128)S(1)} %get-tuple-element.149) | copy-start | bytes 24580
  76.0 236.6 %copy-start.58 = (f32[1,1,1,2048]{3,1,2,0:T(1,128)}, f32[1,1,1,2048]{3,1,2,0:T(1,128)S(1)}, u32[]{:S(2)}) copy-start(f32[1,1,1,2048]{3,1,2,0:T(1,128)S(1)} %get-tuple-element.150) | copy-start | bytes 24580
  76.0 236.6 %copy-start.76 = (f32[1,1,1,2048]{3,1,2,0:T(1,128)}, f32[1,1,1,2048]{3,1,2,0:T(1,128)S(1)}, u32[]{:S(2)}) copy-start(f32[1,1,1,2048]{3,1,2,0:T(1,128)S(1)} %get-tuple-element.151) | copy-start | bytes 24580
  141.0 53.0 %copy-start.52 = (bf16[512,2,32]{2,0,1:T(8,128)(2,1)}, bf16[512,2,32]{2,0,1:T(8,128)(2,1)S(1)}, u32[]{:S(2)}) copy-start(bf16[512,2,32]{2,0,1:T(8,128)(2,1)S(1)} %get-tuple-element.129) | copy-start | bytes 196612
  142.3 58.0 %all-gather.35.cloned.1.call-start = ((), (), s32[]{:S(2)}) async-start(), calls=%async_computation.23 | async-start | bytes 1572864 | tf_op jit(solution)/shard_map/all_gather | solution.py:123
  144.5 168.1 %all-gather.39.cloned.1.call-start = ((), (), s32[]{:S(2)}) async-start(), calls=%async_computation.25 | async-start | bytes 9437184 | tf_op jit(solution)/shard_map/all_gather | solution.py:298
  156.4 281.7 %all-gather.41.cloned.1.call-start = ((), (), s32[]{:S(2)}) async-start(), calls=%async_computation.26 | async-start | bytes 9437184 | tf_op jit(solution)/shard_map/all_gather | solution.py:299
  167.4 321.8 %all-gather.37.cloned.1.call-start = ((), (), s32[]{:S(2)}) async-start(), calls=%async_computation.24 | async-start | bytes 2359296 | tf_op jit(solution)/shard_map/all_gather | solution.py:297
  170.4 432.8 %all-gather.43.cloned.1.call-start = ((), (), s32[]{:S(2)}) async-start(), calls=%async_computation.27 | async-start | bytes 7077888 | tf_op jit(solution)/shard_map/all_gather | solution.py:296
  171.1 472.5 %all-gather.47.cloned.1.call-start = ((), (), s32[]{:S(2)}) async-start(), calls=%async_computation.29 | async-start | bytes 2359296 | tf_op jit(solution)/shard_map/all_gather | solution.py:297
  171.9 597.1 %all-gather.49.cloned.1.call-start = ((), (), s32[]{:S(2)}) async-start(), calls=%async_computation.30 | async-start | bytes 9437184 | tf_op jit(solution)/shard_map/all_gather | solution.py:298
  172.6 721.4 %all-gather.51.cloned.1.call-start = ((), (), s32[]{:S(2)}) async-start(), calls=%async_computation.31 | async-start | bytes 9437184 | tf_op jit(solution)/shard_map/all_gather | solution.py:299
  173.2 742.5 %all-gather.31.cloned.1.call-start = ((), (), s32[]{:S(2)}) async-start(), calls=%async_computation.12 | async-start | bytes 1572864 | tf_op jit(solution)/shard_map/all_gather | solution.py:122
  191.3 121.3 %copy-start.84 = (f32[1,1,2048]{2,1,0:T(1,128)}, f32[1,1,2048]{2,1,0:T(1,128)S(1)}, u32[]{:S(2)}) copy-start(f32[1,1,2048]{2,1,0:T(1,128)S(1)} %convert_element_type.508) | copy-start | bytes 24580
  203.9 285.3 %copy-start.36 = (bf16[2,256,512]{2,1,0:T(8,128)(2,1)}, bf16[2,256,512]{2,1,0:T(8,128)(2,1)S(1)}, u32[]{:S(2)}) copy-start(bf16[2,256,512]{2,1,0:T(8,128)(2,1)S(1)} %fusion.177) | copy-start | bytes 1572868
  493.4 7.2 collective-permute-start
  503.4 92.9 %collective-permute-start.1 = (f32[1,512,2048]{2,1,0:T(8,128)}, f32[1,512,2048]{2,1,0:T(8,128)}, u32[]{:S(2)}, u32[]{:S(2)}) collective-permute-start(f32[1,512,2048]{2,1,0:T(8,128)} %add.364), channel_id=1, source_target_pairs={{0,16},{8,24},{16,0},{24,8},{1,17},{9,25},{17,1},{25,9},{2,18},{10... | collective-permute-start | bytes 12582920 | tf_op jit(solution)/shard_map/ppermute | solution.py:23
  565.6 37.6 %copy-start.82 = (f32[1,1,1,2048]{3,1,2,0:T(1,128)}, f32[1,1,1,2048]{3,1,2,0:T(1,128)S(1)}, u32[]{:S(2)}) copy-start(f32[1,1,1,2048]{3,1,2,0:T(1,128)S(1)} %get-tuple-element.145) | copy-start | bytes 24580
  565.7 203.3 %copy-start.80 = (f32[1,1,1,2048]{3,1,2,0:T(1,128)}, f32[1,1,1,2048]{3,1,2,0:T(1,128)S(1)}, u32[]{:S(2)}) copy-start(f32[1,1,1,2048]{3,1,2,0:T(1,128)S(1)} %get-tuple-element.147) | copy-start | bytes 24580
  613.9 29.7 %copy-start.13 = (bf16[1,512,2048]{2,1,0:T(8,128)(2,1)S(1)}, bf16[1,512,2048]{2,1,0:T(8,128)(2,1)}, u32[]{:S(2)}) copy-start(bf16[1,512,2048]{2,1,0:T(8,128)(2,1)} %param.10) | copy-start | bytes 6291460
  620.6 317.8 %all-gather.45.cloned.1.call-start = ((), (), s32[]{:S(2)}) async-start(), calls=%async_computation.28 | async-start | bytes 1572864 | tf_op jit(solution)/shard_map/all_gather | solution.py:123
  650.9 323.5 %reduce-scatter.18.cloned.1.call-start = ((), (), s32[]{:S(2)}) async-start(), calls=%async_computation.14 | async-start | bytes 1572864 | tf_op jit(solution)/shard_map/reduce_scatter | solution.py:228
  922.5 61.6 %reduce-scatter.16.cloned.1.call-start = ((), (), s32[]{:S(2)}) async-start(), calls=%async_computation.13 | async-start | bytes 1572864 | tf_op jit(solution)/shard_map/reduce_scatter | solution.py:225
  946.1 42.8 %collective-permute-start.2 = (f32[1,512,2048]{2,1,0:T(8,128)}, f32[1,512,2048]{2,1,0:T(8,128)}, u32[]{:S(2)}, u32[]{:S(2)}) collective-permute-start(f32[1,512,2048]{2,1,0:T(8,128)} %add_bitcast_fusion), channel_id=1, source_target_pairs={{0,8},{8,0},{16,24},{24,16},{1,9},{9,1},{17,25},{25,17},{2,10},{10... | collective-permute-start | bytes 12582920 | tf_op jit(solution)/shard_map/ppermute | solution.py:23
  952.1 203.6 %all-reduce.7.cloned.1.call-start = ((), (), s32[]{:S(2)}) async-start(), calls=%async_computation.35 | async-start | bytes 8388608 | tf_op jit(solution)/shard_map/psum | solution.py:252
  995.6 169.8 %collective-permute-start.3 = (f32[1,512,2048]{2,1,0:T(8,128)}, f32[1,512,2048]{2,1,0:T(8,128)}, u32[]{:S(2)}, u32[]{:S(2)}) collective-permute-start(f32[1,512,2048]{2,1,0:T(8,128)} %add.385), channel_id=1, source_target_pairs={{0,16},{8,24},{16,0},{24,8},{1,17},{9,25},{17,1},{25,9},{2,18},{10... | collective-permute-start | bytes 12582920 | tf_op jit(solution)/shard_map/ppermute | solution.py:23
  1004.4 210.1 %reduce-scatter.22.cloned.1.call-start = ((), (), s32[]{:S(2)}) async-start(), calls=%async_computation.16 | async-start | bytes 1572864 | tf_op jit(solution)/shard_map/reduce_scatter | solution.py:228
  1180.7 43.6 %reduce-scatter.20.cloned.1.call-start = ((), (), s32[]{:S(2)}) async-start(), calls=%async_computation.15 | async-start | bytes 1572864 | tf_op jit(solution)/shard_map/reduce_scatter | solution.py:225
  1191.2 140.7 %all-reduce.5.cloned.1.call-start = ((), (), s32[]{:S(2)}) async-start(), calls=%async_computation.34 | async-start | bytes 8388608 | tf_op jit(solution)/shard_map/psum | solution.py:251
  1230.7 15.5 copy-start.24
  1246.2 161.6 %reduce-scatter.36.cloned.1.call-start = ((), (), s32[]{:S(2)}) async-start(), calls=%async_computation.33 | async-start | bytes 589824
  1261.0 72.8 %copy-start.3 = (bf16[1,512,2048]{2,1,0:T(8,128)(2,1)S(1)}, bf16[1,512,2048]{2,1,0:T(8,128)(2,1)}, u32[]{:S(2)}) copy-start(bf16[1,512,2048]{2,1,0:T(8,128)(2,1)} %param.9) | copy-start | bytes 6291460
  1261.1 72.8 %copy-start.57 = (f32[1,1,1,2048]{3,1,2,0:T(1,128)S(1)}, f32[1,1,1,2048]{3,1,2,0:T(1,128)}, u32[]{:S(2)}) copy-start(f32[1,1,1,2048]{3,1,2,0:T(1,128)} %copy-done.56) | copy-start | bytes 24580
  1261.1 72.8 %copy-start.59 = (f32[1,1,1,2048]{3,1,2,0:T(1,128)S(1)}, f32[1,1,1,2048]{3,1,2,0:T(1,128)}, u32[]{:S(2)}) copy-start(f32[1,1,1,2048]{3,1,2,0:T(1,128)} %copy-done.58) | copy-start | bytes 24580
  1261.1 72.8 %copy-start.63 = (f32[512]{0:T(512)S(1)}, f32[512]{0:T(512)}, u32[]{:S(2)}) copy-start(f32[512]{0:T(512)} %copy-done.62) | copy-start | bytes 6148
  1261.1 201.0 %reduce-scatter.34.cloned.1.call-start = ((), (), s32[]{:S(2)}) async-start(), calls=%async_computation.32 | async-start | bytes 147456
  1263.7 255.9 %reduce-scatter.32.cloned.1.call-start = ((), (), s32[]{:S(2)}) async-start(), calls=%async_computation.21 | async-start | bytes 73728 | tf_op jit(solution)/shard_map/reduce_scatter | solution.py:361
  1345.8 265.8 %reduce-scatter.26.cloned.1.call-start = ((), (), s32[]{:S(2)}) async-start(), calls=%async_computation.18 | async-start | bytes 4718592 | tf_op jit(solution)/shard_map/reduce_scatter | solution.py:331
  1350.5 472.8 %reduce-scatter.24.cloned.1.call-start = ((), (), s32[]{:S(2)}) async-start(), calls=%async_computation.17 | async-start | bytes 14155776 | tf_op jit(solution)/shard_map/reduce_scatter | solution.py:325
  1367.5 738.1 %reduce-scatter.28.cloned.1.call-start = ((), (), s32[]{:S(2)}) async-start(), calls=%async_computation.19 | async-start | bytes 18874368 | tf_op jit(solution)/shard_map/reduce_scatter | solution.py:337
  1388.1 1000.7 %reduce-scatter.30.cloned.1.call-start = ((), (), s32[]{:S(2)}) async-start(), calls=%async_computation.20 | async-start | bytes 18874368 | tf_op jit(solution)/shard_map/reduce_scatter | solution.py:343
  (71 other events, 294.7 us)
Sparse Core Ops, SparseCore 0:
  17.8 104.9 all-gather.32
  142.4 19.4 all-gather.28
  164.1 21.3 all-gather.34
  188.0 124.4 all-gather.38
  315.0 123.1 all-gather.40
  440.6 48.5 all-gather.36
  491.8 100.9 all-gather.42
  594.9 48.6 all-gather.46
  646.3 122.6 all-gather.48
  770.9 123.1 all-gather.50
  896.1 19.4 all-gather.30
  917.0 21.2 all-gather.44
  941.2 20.3 reduce-scatter.17
  963.7 20.3 reduce-scatter.15
  1004.6 151.0 all-reduce.6
  1180.9 20.3 reduce-scatter.21
  1203.9 20.3 reduce-scatter.19
  1246.4 85.4 all-reduce.4
  1335.2 62.7 reduce-scatter.35
  1401.2 60.8 reduce-scatter.33
  1465.8 53.7 reduce-scatter.31
  1523.8 87.7 reduce-scatter.25
  1615.8 207.4 reduce-scatter.23
  1826.9 278.6 reduce-scatter.27
  2109.4 279.2 reduce-scatter.29
